TPU v7x, 32 devices: a whole 2x2x4 slice. The times are simulated.
32 devices in a mesh: parts: 2 (over x), seq: 16 (over z, y, core).
Axes of the slice: x: 2, y: 2, z: 4, core: 2. Of those that a mesh axis runs over, the one named last changes fastest.
Arguments:
- token_ids: int32 [4, 4], P(None, 'parts'), parts along dimension 1, may hold values from 0 to 76031
- lengths: int32 [4], P('parts'), parts along dimension 0, may hold values from 24576 to 32768, as said below
- embed_table: bfloat16 [76032, 5120], P('seq'), may hold values from -6 to 6
- attn_gain: bfloat16 [5120], replicated, may hold values from 0.25 to 1.75
- w_qkv: bfloat16 [5120, 7168], P('seq'), may hold values from -0.125 to 0.125
- qkv_bias: float32 [7168], replicated, may hold values from -8 to 8
- cache_keys: bfloat16 [4, 32768, 1024], P('parts', 'seq'), parts along dimension 0, may hold values from -300 to 300
- cache_values: bfloat16 [4, 32768, 1024], P('parts', 'seq'), parts along dimension 0, may hold values from -6 to 6
- w_out: bfloat16 [5120, 5120], P(None, 'seq'), may hold values from -0.078125 to 0.078125
- mlp_gain: bfloat16 [5120], replicated, may hold values from 0.25 to 1.75
- w_gate: bfloat16 [5120, 16384], P(None, 'seq'), may hold values from -0.078125 to 0.078125
- w_up: bfloat16 [5120, 16384], P(None, 'seq'), may hold values from -0.078125 to 0.078125
- w_down: bfloat16 [16384, 5120], P('seq'), may hold values from -0.0625 to 0.0625
Outputs:
- attended: bfloat16 [4, 4, 5120], P(None, 'parts'), parts along dimension 1
- layer_out: bfloat16 [4, 4, 5120], P(None, 'parts', 'seq'), parts along dimension 1
There are 2 independent parts, one for each index of `parts`. A program takes and returns all parts, laid end to end along the dimension named above; an argument that names none is the same for every part. Nothing has to cross between parts.
Inputs may be any that keep to these rules, and one draw needn't show every extreme that they name: Cache positions lengths[b] and later are unused; the first prompt fills the whole cache of 32768 positions.
All inputs are finite; a program needn't handle non-finite values.
Results may differ from a plain program's by a relative error of at most 0.017.
The roundings to bfloat16 on the way count: a program that leaves them out, or rounds other values in their place, can miss the bound.
Values may be sent and summed in bfloat16 or wider, within the bound.
A program may use at most 192 MiB of HBM per device.

v0:
```python
import math

import jax
import jax.numpy as jnp
from jax import lax
from jax.sharding import PartitionSpec as P

HEADS = 40
KV_HEADS = 8
HEAD_DIM = 128


NORM_EPS = 1e-06
ROPE_BASE = 1000000.0
MASKED = -1e30


def joined_2(part, axis, combine):
    gathered = jax.tree.map(lambda a: lax.all_gather(a, axis), part)

    def take(source):
        return jax.tree.map(lambda a: lax.dynamic_index_in_dim(a, source, 0, False), gathered)

    return lax.fori_loop(
        1, lax.axis_size(axis), lambda source, state: combine(state, take(source)), take(0)
    )


def rms_normalize(rows, gain):
    mean_square = jnp.mean(rows * rows, axis=-1, keepdims=True)
    return (rows * lax.rsqrt(mean_square + NORM_EPS) * gain.astype(jnp.float32)).astype(
        jnp.bfloat16
    )


def rotate(vectors, positions):
    half_dim = vectors.shape[-1] // 2
    frequency = ROPE_BASE ** (-2.0 * jnp.arange(half_dim, dtype=jnp.float32) / vectors.shape[-1])
    angles = positions.astype(jnp.float32)[..., None, None] * frequency
    cosine = jnp.cos(angles)
    sine_part = jnp.sin(angles)
    widened = vectors.astype(jnp.float32)
    first_half = widened[..., :half_dim]
    second = widened[..., half_dim:]
    joined = jnp.concatenate(
        [first_half * cosine - second * sine_part, second * cosine + first_half * sine_part],
        axis=-1,
    )
    return joined.astype(jnp.bfloat16)


def combine_partials(earlier, latter):
    top_one, total_one, sum_one = earlier
    top_two, total_two, sum_two = latter
    joined_top = jnp.maximum(top_one, top_two)
    scale_one = jnp.exp(top_one - joined_top)
    scale_two = jnp.exp(top_two - joined_top)
    return (
        joined_top,
        total_one * scale_one + total_two * scale_two,
        sum_one * scale_one[..., None] + sum_two * scale_two[..., None],
    )


def body(
    token_ids,
    lengths,
    embed_table,
    attn_gain,
    w_qkv,
    qkv_bias,
    cache_keys,
    cache_values,
    w_out,
    mlp_gain,
    w_gate,
    w_up,
    w_down,
):
    rank = lax.axis_index("seq")
    step_count, batch_count = token_ids.shape
    model_width = embed_table.shape[1]
    vocab_rows = embed_table.shape[0]
    query_width = HEADS * HEAD_DIM
    key_width = KV_HEADS * HEAD_DIM
    group_size = HEADS // KV_HEADS
    local_ids = token_ids - rank * vocab_rows
    inside = (local_ids >= 0) & (local_ids < vocab_rows)
    picked = jnp.take(embed_table, jnp.clip(local_ids, 0, vocab_rows - 1), axis=0)
    partial_rows = jnp.where(inside[..., None], picked.astype(jnp.float32), 0.0)
    stream = lax.psum(partial_rows, "seq")
    normed = rms_normalize(stream, attn_gain).reshape(-1, model_width)
    feature_rows = w_qkv.shape[0]
    normed_local = lax.dynamic_slice_in_dim(normed, rank * feature_rows, feature_rows, 1)
    joint_partial = jnp.dot(normed_local, w_qkv, preferred_element_type=jnp.float32)
    joint_summed = lax.psum(joint_partial, "seq")
    joint = (joint_summed + qkv_bias).astype(jnp.bfloat16).reshape(step_count, batch_count, -1)
    query_part = joint[..., :query_width].reshape(step_count, batch_count, HEADS, HEAD_DIM)
    key_part = joint[..., query_width : query_width + key_width].reshape(
        step_count, batch_count, KV_HEADS, HEAD_DIM
    )
    value_part = joint[..., query_width + key_width :].reshape(
        step_count, batch_count, KV_HEADS, HEAD_DIM
    )
    positions = lengths[None, :] + jnp.arange(step_count, dtype=jnp.int32)[:, None]
    queries = rotate(query_part, positions)
    new_keys = rotate(key_part, positions)
    grouped = queries.reshape(step_count, batch_count, KV_HEADS, group_size, HEAD_DIM)
    score_scale = 1.0 / math.sqrt(HEAD_DIM)
    local_len = cache_keys.shape[1]
    key_blocks = cache_keys.reshape(batch_count, local_len, KV_HEADS, HEAD_DIM)
    value_blocks = cache_values.reshape(batch_count, local_len, KV_HEADS, HEAD_DIM)
    scores = (
        jnp.einsum("sbkgd,bpkd->bkgsp", grouped, key_blocks, preferred_element_type=jnp.float32)
        * score_scale
    )
    places = rank * local_len + jnp.arange(local_len, dtype=jnp.int32)
    valid = (places[None, :] < lengths[:, None])[:, None, None, None, :]
    masked = jnp.where(valid, scores, MASKED)
    local_top = jnp.max(masked, axis=-1)
    weights = jnp.where(valid, jnp.exp(masked - local_top[..., None]), 0.0)
    local_total = jnp.sum(weights, axis=-1)
    local_sum = jnp.einsum(
        "bkgsp,bpkd->bkgsd",
        weights.astype(jnp.bfloat16),
        value_blocks,
        preferred_element_type=jnp.float32,
    )
    merged_top, merged_total, merged_sum = joined_2(
        (local_top, local_total, local_sum), "seq", combine_partials
    )
    new_scores = (
        jnp.einsum("sbkgd,tbkd->bkgst", grouped, new_keys, preferred_element_type=jnp.float32)
        * score_scale
    )
    step_index = jnp.arange(step_count, dtype=jnp.int32)
    causal = step_index[:, None] >= step_index[None, :]
    new_masked = jnp.where(causal, new_scores, MASKED)
    final_top = jnp.maximum(merged_top, jnp.max(new_masked, axis=-1))
    rescale = jnp.exp(merged_top - final_top)
    new_weights = jnp.where(causal, jnp.exp(new_masked - final_top[..., None]), 0.0)
    final_total = merged_total * rescale + jnp.sum(new_weights, axis=-1)
    final_sum = merged_sum * rescale[..., None] + jnp.einsum(
        "bkgst,tbkd->bkgsd",
        new_weights.astype(jnp.bfloat16),
        value_part,
        preferred_element_type=jnp.float32,
    )
    attended = jnp.transpose(final_sum / final_total[..., None], (3, 0, 1, 2, 4))
    attended = attended.reshape(step_count, batch_count, query_width).astype(jnp.bfloat16)
    shard_cols = w_out.shape[1]
    projected = jnp.dot(
        attended.reshape(-1, query_width), w_out, preferred_element_type=jnp.float32
    )
    stream_shard = lax.dynamic_slice_in_dim(stream, rank * shard_cols, shard_cols, 2)
    mid_shard = stream_shard + projected.reshape(step_count, batch_count, shard_cols)
    squares = lax.psum(jnp.sum(mid_shard * mid_shard, axis=-1), "seq")
    row_scale = lax.rsqrt(squares / model_width + NORM_EPS)
    gain_shard = lax.dynamic_slice_in_dim(mlp_gain, rank * shard_cols, shard_cols, 0).astype(
        jnp.float32
    )
    normed_shard = (mid_shard * row_scale[..., None] * gain_shard).astype(jnp.bfloat16)
    normed_mid = lax.all_gather(normed_shard, "seq", axis=2, tiled=True)
    flat_rows = normed_mid.reshape(-1, model_width)
    gate = jnp.dot(flat_rows, w_gate, preferred_element_type=jnp.float32)
    upper = jnp.dot(flat_rows, w_up, preferred_element_type=jnp.float32)
    hidden = (jax.nn.silu(gate) * upper).astype(jnp.bfloat16)
    down_terms = jnp.dot(hidden, w_down, preferred_element_type=jnp.float32).reshape(
        step_count, batch_count, model_width
    )
    summed = lax.psum_scatter(down_terms, "seq", scatter_dimension=2, tiled=True)
    layer_out = (mid_shard + summed).astype(jnp.bfloat16)
    return (attended, layer_out)


def solution(mesh):
    return jax.shard_map(
        body,
        mesh=mesh,
        in_specs=(
            P(None, "parts"),
            P("parts"),
            P("seq", None),
            P(),
            P("seq", None),
            P(),
            P("parts", "seq", None),
            P("parts", "seq", None),
            P(None, "seq"),
            P(),
            P(None, "seq"),
            P(None, "seq"),
            P("seq", None),
        ),
        out_specs=(P(None, "parts", None), P(None, "parts", "seq")),
        check_vma=False,
    )
```

profile of v0, /device:TPU:0, one launch (start us, length us, event | category | flops | bytes accessed | tf_op | source)
XLA Modules:
  0.0 495.7 jit_solution(8823497209833906688)
XLA Ops:
  13.4 8.8 %copy.106 = bf16[512,8,8,128]{3,2,1,0:T(8,128)(2,1)} copy(bf16[512,8,8,128]{3,1,2,0:T(8,128)(2,1)} %bitcast.100) | data formatting | bytes 16777216
  22.2 7.1 %bitcast_bitcast_fusion.1 = bf16[2,2048,8,128,1]{3,2,1,0,4:T(8,128)(2,1)} fusion(bf16[2,2048,8,128]{3,2,1,0:T(8,128)(2,1)} %bitcast.97), kind=kLoop, calls=%fused_computation.12 | loop fusion | bytes 16777216 | tf_op jit(solution)/shard_map/reshape | solution.py:111
  29.3 8.8 %copy.107 = bf16[512,8,8,128]{3,2,1,0:T(8,128)(2,1)} copy(bf16[512,8,8,128]{3,1,2,0:T(8,128)(2,1)} %bitcast.101) | data formatting | bytes 16777216
  38.1 7.0 %bitcast_bitcast_fusion = bf16[2,2048,8,128,1]{3,2,1,0,4:T(8,128)(2,1)} fusion(bf16[2,2048,8,128]{3,2,1,0:T(8,128)(2,1)} %bitcast.98), kind=kLoop, calls=%fused_computation.11 | loop fusion | bytes 16777216 | tf_op jit(solution)/shard_map/reshape | solution.py:112
  45.1 58.0 %all-reduce.3.cloned.1.call-done = f32[4,2,5120]{2,1,0:T(2,128)} async-done(((f32[4,2,5120]{2,1,0:T(2,128)}), f32[4,2,5120]{2,1,0:T(2,128)}) %all-reduce.3.cloned.1.call-update) | async-done | bytes 163856 | tf_op jit(solution)/shard_map/psum | solution.py:91
  105.3 3.7 fusion.47
  109.4 90.0 %all-reduce.5.cloned.1.call-done = f32[8,7168]{1,0:T(8,128)} async-done(((f32[8,7168]{1,0:T(8,128)}), f32[8,7168]{1,0:T(8,128)}) %all-reduce.5.cloned.1.call-update) | async-done | bytes 229392 | tf_op jit(solution)/shard_map/psum | solution.py:96
  201.2 6.3 %bitcast_reduce_fusion = (f32[2,8,5,4]{2,3,1,0:T(4,128)S(1)}, f32[2,8,4,5,2048]{4,3,2,1,0:T(8,128)S(1)}) fusion(pred[2,2048]{1,0:T(4,128)(4,1)S(1)} %broadcast_compare_fusion, bf16[2,2048,8,128,1]{3,2,1,0,4:T(8,128)(2,1)} %bitcast_bitcast_fusion.1, bf16[4,2,8,5,64]{4,3,0,2,1:T(8,128)(2,1)S(1)} %copy.69, bf16[4,2,8,5,64]{4,3,0,2,1:T(8,128)(2,1)S(1)} %copy.68), kind=kOutput, calls=%fused_computation.18 | convolution fusion | flops 169901760 | bytes 11097344 | tf_op jit(solution)/shard_map/sbkgd,bpkd->bkgsp/dot_general | solution.py:114
  207.6 3.1 fusion.4
  212.5 3.6 fusion.13
  216.2 23.1 %all-gather.1 = f32[32,8,5,4]{1,3,2,0:T(4,128)S(1)} all-gather(f32[2,8,5,4]{1,3,2,0:T(4,128)S(1)} %copy.72), channel_id=3, replica_groups=mesh['parts'=2,'seq'=16] {'seq'}, dimensions={0}, use_global_device_ids=true | all-gather | bytes 21760 | tf_op jit(solution)/shard_map/all_gather | solution.py:19
  240.1 19.3 %all-gather = f32[32,8,5,4]{1,3,2,0:T(4,128)S(1)} all-gather(f32[2,8,5,4]{1,3,2,0:T(4,128)S(1)} %copy.71), channel_id=2, replica_groups=mesh['parts'=2,'seq'=16] {'seq'}, dimensions={0}, use_global_device_ids=true | all-gather | bytes 21760 | tf_op jit(solution)/shard_map/all_gather | solution.py:19
  261.1 2.3 fusion.60
  265.1 57.2 %while.19 = (s32[]{:T(128)}, f32[2,8,5,4]{1,3,2,0:T(4,128)S(1)}, f32[2,8,5,4]{1,3,2,0:T(4,128)S(1)}, f32[2,8,5,4,128]{4,3,2,1,0:T(4,128)}, f32[16,2,8,5,4]{2,4,3...) while((s32[]{:T(128)}, f32[2,8,5,4]{1,3,2,0:T(4,128)S(1)}, ...), condition=%wide.region_6.7_spmd, body=%wide.region_5.6_spmd.sunk | while | flops 124805 | bytes 837271 | solution.py:24
  267.0 1.8 fusion.72
  270.9 1.8 fusion.72
  274.7 1.8 fusion.72
  278.5 1.8 fusion.72
  282.3 1.8 fusion.72
  286.1 1.8 fusion.72
  290.0 1.8 fusion.72
  293.8 1.8 fusion.72
  325.1 1.8 multiply_reduce_fusion.1
  327.0 30.7 %psum.23 = f32[4,2]{1,0:T(4,128)S(1)} all-reduce(f32[4,2]{1,0:T(4,128)S(1)} %get-tuple-element.245), channel_id=1, replica_groups=mesh['parts'=2,'seq'=16] {'seq'}, use_global_device_ids=true, to_apply=%region_10.11 | all-reduce | flops 8 | bytes 64 | tf_op jit(solution)/shard_map/psum | solution.py:157
  357.9 33.2 %all_gather.27 = bf16[4,2,5120]{0,1,2:T(2,128)(2,1)} all-gather(bf16[4,2,320]{0,1,2:T(2,128)(2,1)S(1)} %copy.85), channel_id=1, replica_groups=mesh['parts'=2,'seq'=16] {'seq'}, dimensions={2}, use_global_device_ids=true | all-gather | bytes 87040 | tf_op jit(solution)/shard_map/all_gather | solution.py:163
  391.2 5.2 %copy.86 = bf16[4,2,5120]{2,1,0:T(2,128)(2,1)S(1)} copy(bf16[4,2,5120]{0,1,2:T(2,128)(2,1)} %all_gather.27) | data formatting | bytes 163840 | tf_op jit(solution)/shard_map/all_gather | solution.py:163
  396.5 5.4 %fusion.61 = f32[8,1024]{1,0:T(8,128)S(1)} fusion(bf16[8,5120]{1,0:T(8,128)(2,1)S(1)} %reshape.133, bf16[5120,1024]{1,0:T(8,128)(2,1)} %param.25), kind=kOutput, calls=%fused_computation.105 | convolution fusion | flops 83886080 | bytes 10600448 | tf_op jit(solution)/shard_map/dot_general | solution.py:165
  401.9 9.8 %fusion.30 = f32[8,5120]{1,0:T(8,128)S(1)} fusion(bf16[1024,5120]{1,0:T(8,128)(2,1)} %param.27, bf16[8,5120]{1,0:T(8,128)(2,1)S(1)} %reshape.133, bf16[5120,1024]{1,0:T(8,128)(2,1)} %param.26, f32[8,1024]{1,0:T(8,128)S(1)} %fusion.61), kind=kOutput, calls=%fused_computation.42 | convolution fusion | flops 167821312 | bytes 21250048 | tf_op jit(solution)/shard_map/dot_general | solution.py:168
  412.5 5.9 %copy.99 = f32[4,2,5120]{0,1,2:T(2,128)} copy(f32[4,2,5120]{2,1,0:T(2,128)} %reshape.134) | data formatting | bytes 327680
  418.4 6.0 %reshape.161 = f32[5120,8]{1,0:T(8,128)} reshape(f32[5120,2,4]{2,1,0:T(2,128)} %bitcast.99) | data formatting | bytes 327680
  424.4 61.2 %reduce-scatter.4.cloned.1.call-done = f32[320,8]{1,0:T(8,128)} async-done(((f32[5120,8]{1,0:T(8,128)}), f32[320,8]{1,0:T(8,128)}) %reduce-scatter.4.cloned.1.call-update) | async-done | bytes 10256
  485.5 1.9 reshape.162
  (157 shorter events, 64.5 us)
Async XLA Ops:
  7.2 317.9 %copy-start = (bf16[5120,320]{0,1:T(8,128)(2,1)S(1)}, bf16[5120,320]{0,1:T(8,128)(2,1)}, u32[]{:S(2)}) copy-start(bf16[5120,320]{0,1:T(8,128)(2,1)} %param.23) | copy-start | bytes 9830404
  7.2 95.9 %all-reduce.3.cloned.1.call-start = ((), (), s32[]{:S(2)}) async-start(), calls=%async_computation.1 | async-start | bytes 327680 | tf_op jit(solution)/shard_map/psum | solution.py:91
  11.2 188.3 %all-reduce.5.cloned.1.call-start = ((), (), s32[]{:S(2)}) async-start(), calls=%async_computation.2 | async-start | bytes 458752 | tf_op jit(solution)/shard_map/psum | solution.py:96
  45.1 154.3 %copy-start.9 = (f32[7168]{0:T(1024)S(1)}, f32[7168]{0:T(1024)}, u32[]{:S(2)}) copy-start(f32[7168]{0:T(1024)} %param.20) | copy-start | bytes 86020
  109.1 154.3 %all-gather.5.cloned.1.call-start = ((), (), s32[]{:S(2)}) async-start(), calls=%async_computation.3 | async-start | bytes 2785280 | tf_op jit(solution)/shard_map/all_gather | solution.py:19
  200.4 0.7 copy-start.5
  201.1 6.5 %slice-start = ((s8[8388608]{0:T(1024)(128)(4,1)}), s8[4194304]{0:T(1024)(128)(4,1)S(1)}, s32[]{:S(2)}) async-start(s8[8388608]{0:T(1024)(128)(4,1)} %bitcast.102), calls=%async_computation.5 | async-start | bytes 8388608
  201.2 6.4 %copy-start.4 = (bf16[4,2,8,5,64]{4,3,0,2,1:T(8,128)(2,1)}, bf16[4,2,8,5,64]{4,3,0,2,1:T(8,128)(2,1)S(1)}, u32[]{:S(2)}) copy-start(bf16[4,2,8,5,64]{4,3,0,2,1:T(8,128)(2,1)S(1)} %copy.69) | copy-start | bytes 122884
  201.2 6.4 %slice-start.1 = ((s8[8388608]{0:T(1024)(128)(4,1)}), s8[4194304]{0:T(1024)(128)(4,1)S(1)}, s32[]{:S(2)}) async-start(s8[8388608]{0:T(1024)(128)(4,1)} %bitcast.102), calls=%async_computation.6 | async-start | bytes 8388608
  207.5 3.2 copy-start.1
  211.5 274.0 %reduce-scatter.4.cloned.1.call-start = ((), (), s32[]{:S(2)}) async-start(), calls=%async_computation.4 | async-start | bytes 2785280
  239.3 0.7 copy-start.2
  259.4 0.7 copy-start.3
  325.1 32.6 %copy-start.6 = (bf16[4,2,5120]{2,1,0:T(2,128)(2,1)}, bf16[4,2,5120]{2,1,0:T(2,128)(2,1)S(1)}, u32[]{:S(2)}) copy-start(bf16[4,2,5120]{2,1,0:T(2,128)(2,1)S(1)} %convert_element_type.77) | copy-start | bytes 245764
  327.0 30.7 %copy-start.7 = (f32[4,2,320]{2,1,0:T(2,128)}, f32[4,2,320]{2,1,0:T(2,128)S(1)}, u32[]{:S(2)}) copy-start(f32[4,2,320]{2,1,0:T(2,128)S(1)} %get-tuple-element.246) | copy-start | bytes 30724
  418.4 70.1 %copy-start.8 = (f32[4,2,320]{2,1,0:T(2,128)S(1)}, f32[4,2,320]{2,1,0:T(2,128)}, u32[]{:S(2)}) copy-start(f32[4,2,320]{2,1,0:T(2,128)} %copy-done.7) | copy-start | bytes 30724
Sparse Core Ops, SparseCore 0:
  11.4 91.6 all-reduce.2
  109.2 90.1 all-reduce.4
  211.6 46.0 all-gather.4
  424.5 61.0 reduce-scatter.3
where the time goes:
time: 499 us; the launch traced here: 496 us
  waiting for transfers between devices  209 us (42%)
  blocking collectives  106 us (21%)
  local copies, waits for them, and re-layouts  78.3 us (16%)
  other arithmetic  53.3 us (11%)
  matrix products  34 us (7%)
  between operations  14.1 us (3%)
    psum x1, waiting for transfers between devices, body(): joint_summed = lax.psum(joint_partial, 'seq')  90 us
    unnamed x5, waiting for transfers between devices  61.2 us
    psum x1, waiting for transfers between devices, body(): stream = lax.psum(partial_rows, 'seq')  58 us
    all_gather x2, blocking collectives, joined_2(): gathered = jax.tree.map(lambda a: lax.all_gather(a, axis), part)  42.5 us
    all_gather x1, blocking collectives, body(): normed_mid = lax.all_gather(normed_shard, 'seq', axis=2, tiled=True)  33.2 us
    unnamed x29, local copies, waits for them, and re-layouts  33.1 us
    psum x1, blocking collectives, body(): squares = lax.psum(jnp.sum(mid_shard * mid_shard, axis=-1), 'seq')  30.7 us
    add x15, other arithmetic, combine_partials(): sum_one * scale_one[..., None] + sum_two * scale_two[..., None]  27.3 us
  transfers between devices with their start and end apart: 4, of which 3 were waited for; matrix products, arithmetic and copies ran while one was open for 8% of the time, Pallas kernels for 0%

commit v1 on v0

v1 whole, which is shorter than its diff:
```python
import functools
import math

import jax
import jax.numpy as jnp
from jax import lax
from jax.experimental import pallas as pl
from jax.experimental.pallas import tpu as pltpu
from jax.sharding import PartitionSpec as P

HEADS = 40
KV_HEADS = 8
HEAD_DIM = 128

NORM_EPS = 1e-06
ROPE_BASE = 1000000.0
MASKED = -1e30
F32 = jnp.float32
BF16 = jnp.bfloat16
MESH = pl.DeviceIdType.MESH


def layer_kernel(
    n,
    lengths,
    picked,
    inside,
    gain_one,
    bias,
    cos,
    sin,
    gain_two,
    qkv_hbm,
    keys_hbm,
    values_hbm,
    out_hbm,
    gate_hbm,
    up_hbm,
    down_hbm,
    attended_ref,
    layer_ref,
    w_qkv,
    keys,
    values,
    w_out,
    w_gate,
    w_up,
    w_down,
    rows_out,
    rows_in,
    joint_out,
    joint_in,
    heads_all,
    heads_wide,
    part_out,
    part_in,
    attended_all,
    mid_all,
    wide,
    narrow,
    down_out,
    down_in,
    load_sem,
    send_sem,
    recv_sem,
):
    me = lax.axis_index("seq")
    group = HEADS // KV_HEADS
    joint_heads = HEADS + 2 * KV_HEADS
    tokens, width = picked.shape
    batches = keys.shape[0]
    local_len = keys.shape[1]
    cols = w_out.shape[1]
    joint_each = joint_out.shape[1]
    head_each = part_out.shape[1] - 1
    scale = 1.0 / math.sqrt(HEAD_DIM)

    loads = [
        pltpu.make_async_copy(a, b, load_sem.at[i])
        for i, (a, b) in enumerate(
            (
                (qkv_hbm, w_qkv),
                (keys_hbm, keys),
                (values_hbm, values),
                (out_hbm, w_out),
                (gate_hbm, w_gate),
                (up_hbm, w_up),
                (down_hbm, w_down),
            )
        )
    ]
    for load in loads:
        load.start()

    barrier = pltpu.get_barrier_semaphore()

    @pl.loop(1, n)
    def _(d):
        pl.semaphore_signal(
            barrier, inc=1, device_id={"seq": lax.rem(me + d, n)}, device_id_type=MESH
        )

    def copy_to(step, source, target, slot, peer):
        return pltpu.make_async_remote_copy(
            src_ref=source,
            dst_ref=target.at[slot],
            send_sem=send_sem.at[step, peer],
            recv_sem=recv_sem.at[step, slot],
            device_id={"seq": peer},
            device_id_type=MESH,
        )

    def send_all(step, source, target, spread):
        @pl.loop(1, n)
        def _(d):
            peer = lax.rem(me + d, n)
            copy_to(step, source.at[peer if spread else me], target, me, peer).start()

    def receive_all(step, target):
        @pl.loop(1, n)
        def _(d):
            peer = lax.rem(me + d, n)
            copy_to(step, target.at[peer], target, peer, peer).wait_recv()

    def sent_all(step, source, spread):
        @pl.loop(1, n)
        def _(d):
            peer = lax.rem(me + d, n)
            src = source.at[peer if spread else me]
            pltpu.make_async_remote_copy(
                src_ref=src,
                dst_ref=src,
                send_sem=send_sem.at[step, peer],
                recv_sem=recv_sem.at[step, peer],
                device_id={"seq": peer},
                device_id_type=MESH,
            ).wait_send()

    wide[...] = picked[...].astype(F32) * inside[...]
    mean_square = jnp.sum(wide[...] * wide[...], axis=1, keepdims=True) / width
    normed = (wide[...] * lax.rsqrt(mean_square + NORM_EPS) * gain_one[...]).astype(BF16)
    heads_out = jnp.concatenate([wide[...], normed.astype(F32)], axis=0)
    for j in range(n):
        rows_out[j] = heads_out[:, j * cols : (j + 1) * cols].astype(BF16)
    part_out[...] = jnp.zeros_like(part_out)
    pl.semaphore_wait(barrier, n - 1)
    send_all(0, rows_out, rows_in, True)
    rows_in[me] = rows_out[me]
    receive_all(0, rows_in)
    rows = lax.fori_loop(
        1, n, lambda j, acc: acc + rows_in[j].astype(F32), rows_in[0].astype(F32)
    )
    stream = rows[:tokens]
    normed_local = rows[tokens:].astype(BF16)

    loads[0].wait()
    chunk = 4

    @pl.loop(0, joint_heads // chunk)
    def _(c):
        part = jnp.dot(
            normed_local,
            w_qkv[:, pl.ds(pl.multiple_of(c * (chunk * HEAD_DIM), HEAD_DIM), chunk * HEAD_DIM)],
            preferred_element_type=F32,
        )
        for i in range(chunk):
            h = c * chunk + i
            joint_out[h // joint_each, h % joint_each] = part[:, i * HEAD_DIM : (i + 1) * HEAD_DIM]

    for h in range(joint_heads, n * joint_each):
        joint_out[h // joint_each, h % joint_each] = jnp.zeros((tokens, HEAD_DIM), F32)
    send_all(1, joint_out, joint_in, True)
    joint_in[me] = joint_out[me]
    receive_all(1, joint_in)
    joint = lax.fori_loop(1, n, lambda j, acc: acc + joint_in[j], joint_in[0])
    tiles = []
    for i in range(joint_each):
        h = jnp.minimum(me * joint_each + i, joint_heads - 1)
        x = (joint[i] + bias[pl.ds(h, 1), :]).astype(BF16).astype(F32)
        turned = x * cos[...] + pltpu.roll(x, HEAD_DIM // 2, 1) * sin[...]
        is_key = jnp.full(x.shape, h, jnp.int32) < HEADS + KV_HEADS
        tiles.append(jnp.where(is_key, turned, x))
    heads_all[me] = jnp.concatenate(tiles, axis=0).astype(BF16)
    send_all(2, heads_all, heads_all, False)
    receive_all(2, heads_all)
    rows_each = joint_each * tokens

    @pl.loop(0, n)
    def _(j):
        heads_wide[pl.ds(pl.multiple_of(j * rows_each, 8), rows_each), :] = heads_all[j].astype(F32)

    loads[1].wait()
    loads[2].wait()
    group_rows = group * tokens
    row_batch = lax.broadcasted_iota(jnp.int32, (group_rows, 1), 0) % batches
    places = me * local_len + lax.broadcasted_iota(jnp.int32, (1, local_len), 1)
    lane = lax.broadcasted_iota(jnp.int32, (tokens, HEAD_DIM), 1)

    @pl.loop(0, KV_HEADS)
    def _(k):
        q = heads_wide[pl.ds(pl.multiple_of(k * group_rows, 8), group_rows), :].astype(BF16)
        head_cols = pl.ds(pl.multiple_of(k * HEAD_DIM, HEAD_DIM), HEAD_DIM)
        top = total = summed = None
        for b in range(batches):
            valid = places < lengths[b]
            scores = lax.dot_general(
                q, keys[b, :, head_cols], (((1,), (1,)), ((), ())), preferred_element_type=F32
            )
            masked = jnp.where(valid, scores * scale, MASKED)
            own_top = jnp.max(masked, axis=1, keepdims=True)
            weight = jnp.where(valid, jnp.exp(masked - own_top), 0.0)
            own_total = jnp.sum(weight, axis=1, keepdims=True)
            own_sum = jnp.dot(
                weight.astype(BF16), values[b, :, head_cols], preferred_element_type=F32
            )
            if b == 0:
                top, total, summed = own_top, own_total, own_sum
            else:
                here = row_batch == b
                top = jnp.where(here, own_top, top)
                total = jnp.where(here, own_total, total)
                summed = jnp.where(here, own_sum, summed)
        for g in range(group):
            h = k * group + g
            owner, slot = h // head_each, h % head_each
            mine = slice(g * tokens, (g + 1) * tokens)
            part_out[owner, slot] = summed[mine]
            stats = part_out[owner, head_each]
            stats = jnp.where(lane == 2 * slot, top[mine], stats)
            part_out[owner, head_each] = jnp.where(lane == 2 * slot + 1, total[mine], stats)

    send_all(3, part_out, part_in, True)
    part_in[me] = part_out[me]

    row = lax.broadcasted_iota(jnp.int32, (tokens, 1), 0)
    fresh = []
    for i in range(head_each):
        h = jnp.minimum(me * head_each + i, HEADS - 1)
        kv = h // group
        q = heads_wide[pl.ds(pl.multiple_of(h * tokens, 8), tokens), :]
        new_key = heads_wide[pl.ds(pl.multiple_of((HEADS + kv) * tokens, 8), tokens), :]
        new_value = heads_wide[
            pl.ds(pl.multiple_of((HEADS + KV_HEADS + kv) * tokens, 8), tokens), :
        ]
        scores = []
        top = jnp.full((tokens, 1), MASKED, F32)
        for t in range(tokens):
            seen = (row % batches == t % batches) & (row >= t)
            score = jnp.sum(q * new_key[t : t + 1], axis=1, keepdims=True) * scale
            score = jnp.where(seen, score, MASKED)
            scores.append((seen, score))
            top = jnp.maximum(top, score)
        fresh.append((top, scores, new_value))

    receive_all(3, part_in)
    tiles = []
    for i in range(head_each):
        top, scores, new_value = fresh[i]

        def stat(j, which):
            return jnp.broadcast_to(
                part_in[j, head_each][:, 2 * i + which : 2 * i + which + 1], (tokens, HEAD_DIM)
            )

        top = jnp.broadcast_to(top, (tokens, HEAD_DIM))
        top = lax.fori_loop(0, n, lambda j, m: jnp.maximum(m, stat(j, 0)), top)
        total = jnp.zeros((tokens, HEAD_DIM), F32)
        summed = jnp.zeros((tokens, HEAD_DIM), F32)
        for t in range(tokens):
            seen, score = scores[t]
            weight = jnp.where(seen, jnp.exp(score - top), 0.0)
            total += weight
            summed += weight.astype(BF16).astype(F32) * new_value[t : t + 1]

        def merge(j, state):
            total, summed = state
            factor = jnp.exp(stat(j, 0) - top)
            return total + stat(j, 1) * factor, summed + part_in[j, i] * factor

        total, summed = lax.fori_loop(0, n, merge, (total, summed))
        tiles.append(summed / total)
    attended_all[me] = jnp.concatenate(tiles, axis=0).astype(BF16)
    send_all(4, attended_all, attended_all, False)
    receive_all(4, attended_all)
    for h in range(HEADS):
        at = (h % head_each) * tokens
        wide[:, h * HEAD_DIM : (h + 1) * HEAD_DIM] = attended_all[h // head_each].astype(F32)[
            at : at + tokens
        ]
    narrow[...] = wide[...].astype(BF16)
    attended_ref[...] = narrow[...]

    loads[3].wait()
    depth = 512

    def piece(c):
        return pl.ds(pl.multiple_of(c * depth, depth), depth)

    mid = stream + lax.fori_loop(
        0,
        width // depth,
        lambda c, acc: acc
        + jnp.dot(narrow[:, piece(c)], w_out[piece(c), :], preferred_element_type=F32),
        jnp.zeros((tokens, cols), F32),
    )
    mid_all[me] = mid
    send_all(5, mid_all, mid_all, False)
    receive_all(5, mid_all)
    for j in range(n):
        wide[:, j * cols : (j + 1) * cols] = mid_all[j]
    mean_square = jnp.sum(wide[...] * wide[...], axis=1, keepdims=True) / width
    narrow[...] = (wide[...] * lax.rsqrt(mean_square + NORM_EPS) * gain_two[...]).astype(BF16)

    loads[4].wait()
    loads[5].wait()
    units = w_gate.shape[1]

    def both(c, state):
        gate, upper = state
        x = narrow[:, piece(c)]
        return (
            gate + jnp.dot(x, w_gate[piece(c), :], preferred_element_type=F32),
            upper + jnp.dot(x, w_up[piece(c), :], preferred_element_type=F32),
        )

    zero = jnp.zeros((tokens, units), F32)
    gate, upper = lax.fori_loop(0, width // depth, both, (zero, zero))
    hidden = (gate / (1.0 + jnp.exp(-gate)) * upper).astype(BF16)
    loads[6].wait()

    @pl.loop(0, width // depth)
    def _(c):
        wide[:, piece(c)] = jnp.dot(hidden, w_down[:, piece(c)], preferred_element_type=F32)

    for j in range(n):
        down_out[j] = wide[:, j * cols : (j + 1) * cols]
    send_all(6, down_out, down_in, True)
    down_in[me] = down_out[me]
    receive_all(6, down_in)
    summed = lax.fori_loop(1, n, lambda j, acc: acc + down_in[j], down_in[0])
    layer_ref[...] = (mid + summed).astype(BF16)

    sent_all(0, rows_out, True)
    sent_all(1, joint_out, True)
    sent_all(2, heads_all, False)
    sent_all(3, part_out, True)
    sent_all(4, attended_all, False)
    sent_all(5, mid_all, False)
    sent_all(6, down_out, True)


def body(
    token_ids,
    lengths,
    embed_table,
    attn_gain,
    w_qkv,
    qkv_bias,
    cache_keys,
    cache_values,
    w_out,
    mlp_gain,
    w_gate,
    w_up,
    w_down,
):
    n = lax.axis_size("seq")
    rank = lax.axis_index("seq")
    step_count, batch_count = token_ids.shape
    tokens = step_count * batch_count
    width = embed_table.shape[1]
    vocab_rows = embed_table.shape[0]
    cols = w_out.shape[1]
    local_ids = token_ids.reshape(-1) - rank * vocab_rows
    inside = (local_ids >= 0) & (local_ids < vocab_rows)
    picked = embed_table.at[jnp.clip(local_ids, 0, vocab_rows - 1)].get(mode="promise_in_bounds")
    positions = (lengths[None, :] + jnp.arange(step_count, dtype=jnp.int32)[:, None]).reshape(-1)
    half = HEAD_DIM // 2
    frequency = ROPE_BASE ** (-2.0 * jnp.arange(half, dtype=F32) / HEAD_DIM)
    angles = positions.astype(F32)[:, None] * frequency
    cosine, sine = jnp.cos(angles), jnp.sin(angles)
    cos = jnp.concatenate([cosine, cosine], axis=1)
    sin = jnp.concatenate([-sine, sine], axis=1)
    joint_heads = HEADS + 2 * KV_HEADS
    joint_each = -(-joint_heads // n)
    head_each = -(-HEADS // n)
    vmem = pl.BlockSpec(memory_space=pltpu.VMEM)
    hbm = pl.BlockSpec(memory_space=pl.ANY)
    attended, layer_out = pl.pallas_call(
        functools.partial(layer_kernel, n),
        out_shape=(
            jax.ShapeDtypeStruct((tokens, width), BF16),
            jax.ShapeDtypeStruct((tokens, cols), BF16),
        ),
        in_specs=[pl.BlockSpec(memory_space=pltpu.SMEM)] + [vmem] * 7 + [hbm] * 7,
        out_specs=(vmem, vmem),
        scratch_shapes=[
            pltpu.VMEM(a.shape, a.dtype)
            for a in (w_qkv, cache_keys, cache_values, w_out, w_gate, w_up, w_down)
        ]
        + [
            pltpu.VMEM((n, 2 * tokens, cols), BF16),
            pltpu.VMEM((n, 2 * tokens, cols), BF16),
            pltpu.VMEM((n, joint_each, tokens, HEAD_DIM), F32),
            pltpu.VMEM((n, joint_each, tokens, HEAD_DIM), F32),
            pltpu.VMEM((n, joint_each * tokens, HEAD_DIM), BF16),
            pltpu.VMEM((n * joint_each * tokens, HEAD_DIM), F32),
            pltpu.VMEM((n, head_each + 1, tokens, HEAD_DIM), F32),
            pltpu.VMEM((n, head_each + 1, tokens, HEAD_DIM), F32),
            pltpu.VMEM((n, head_each * tokens, HEAD_DIM), BF16),
            pltpu.VMEM((n, tokens, cols), F32),
            pltpu.VMEM((tokens, width), F32),
            pltpu.VMEM((tokens, width), BF16),
            pltpu.VMEM((n, tokens, cols), F32),
            pltpu.VMEM((n, tokens, cols), F32),
            pltpu.SemaphoreType.DMA((7,)),
            pltpu.SemaphoreType.DMA((7, n)),
            pltpu.SemaphoreType.DMA((7, n)),
        ],
        compiler_params=pltpu.CompilerParams(
            collective_id=0, has_side_effects=True, vmem_limit_bytes=67043328
        ),
    )(
        lengths,
        picked,
        inside.astype(F32)[:, None],
        attn_gain.astype(F32)[None, :],
        qkv_bias.reshape(joint_heads, HEAD_DIM),
        cos,
        sin,
        mlp_gain.astype(F32)[None, :],
        w_qkv,
        cache_keys,
        cache_values,
        w_out,
        w_gate,
        w_up,
        w_down,
    )
    return (
        attended.reshape(step_count, batch_count, width),
        layer_out.reshape(step_count, batch_count, cols),
    )


def solution(mesh):
    return jax.shard_map(
        body,
        mesh=mesh,
        in_specs=(
            P(None, "parts"),
            P("parts"),
            P("seq", None),
            P(),
            P("seq", None),
            P(),
            P("parts", "seq", None),
            P("parts", "seq", None),
            P(None, "seq"),
            P(),
            P(None, "seq"),
            P(None, "seq"),
            P("seq", None),
        ),
        out_specs=(P(None, "parts", None), P(None, "parts", "seq")),
        check_vma=False,
    )
```

time: 499 us -> 98.8 us (0.20)
  waiting for transfers between devices: 209 us -> 0 us
  blocking collectives: 106 us -> 0 us
  Pallas kernels: 0 us -> 80 us
  local copies, waits for them, and re-layouts: 78.3 us -> 12.2 us
  other arithmetic: 53.3 us -> 5.45 us
  matrix products: 34 us -> 0 us
  between operations: 14.1 us -> 0.65 us
    psum x2 -> x0, waiting for transfers between devices: 148 us -> none  [the longest x1 90 us: body(): joint_summed = lax.psum(joint_partial, 'seq')]
    pallas_call x0 -> x1, Pallas kernels: none -> 80 us  [body(): pl.pallas_call(functools.partial(layer_kernel, n), out_shape=(jax.ShapeDt...]
    all_gather x3 -> x0, blocking collectives: 75.7 us -> none  [the longest x2 42.5 us: joined_2(): gathered = jax.tree.map(lambda a: lax.all_gather(a, axis), part)]
    unnamed x5 -> x0, waiting for transfers between devices: 61.2 us -> none
    add x32 -> x0, other arithmetic: 39 us -> none  [the longest x15 27.3 us: combine_partials(): sum_one * scale_one[..., None] + sum_two * scale_two[..., None]]
    dot_general x8 -> x0, matrix products: 34 us -> none  [the longest x1 9.79 us: body(): jnp.dot(hidden, w_down, preferred_element_type=jnp.float32)]
    psum x1 -> x0, blocking collectives: 30.7 us -> none  [body(): squares = lax.psum(jnp.sum(mid_shard * mid_shard, axis=-1), 'seq')]
    unnamed x29 -> x1, local copies, waits for them, and re-layouts: 33.1 us -> 5.82 us
  transfers between devices with their start and end apart: 4 -> 0, of which waited for: 3 -> 0; matrix products, arithmetic and copies ran while one was open for 8% -> 0% of each run, Pallas kernels for 0% -> 0%
where the time goes in v1:
time: 98.8 us; the launch traced here: 98.3 us
  Pallas kernels  80 us (81%)
  local copies, waits for them, and re-layouts  12.2 us (12%)
  other arithmetic  5.45 us (6%)
    pallas_call x1, Pallas kernels, body(): pl.pallas_call(functools.partial(layer_kernel, n), out_shape=(jax.ShapeDt...  80 us
    unnamed x1, local copies, waits for them, and re-layouts  5.82 us
    gather x1, local copies, waits for them, and re-layouts, body(): embed_table.at[jnp.clip(local_ids, 0, vocab_rows - 1)]  2.49 us

profile of v1, /device:TPU:0, one launch (start us, length us, event | category | flops | bytes accessed | tf_op | source)
XLA Modules:
  0.0 98.3 jit_solution(13679617239534458603)
XLA Ops:
  0.6 0.7 and_convert_fusion
  1.3 0.7 subtract_clamp_fusion
  2.0 0.1 copy.19
  2.1 0.1 min.12
  2.2 0.1 copy.20
  2.3 0.7 reshape.99.inside
  3.0 0.7 add_convert_fusion
  3.6 0.1 convert_element_type.28
  3.7 0.1 fusion
  3.8 0.7 pad_maximum_fusion
  4.5 1.3 %broadcast_in_dim.20 = f32[5120]{0:T(1024)} convert(bf16[5120]{0:T(1024)(128)(2,1)} %param.16) | non-fusion elementwise | flops 5120 | bytes 30720 | tf_op jit(solution)/shard_map/broadcast_in_dim | solution.py:427
  5.8 1.3 %broadcast_in_dim.21 = f32[5120]{0:T(1024)} convert(bf16[5120]{0:T(1024)(128)(2,1)} %param.22) | non-fusion elementwise | flops 5120 | bytes 30720 | tf_op jit(solution)/shard_map/broadcast_in_dim | solution.py:431
  7.1 2.5 %gather_fusion = bf16[8,5120]{1,0:T(8,128)(2,1)} fusion(bf16[4752,5120]{1,0:T(8,128)(2,1)} %param.15, s32[1024]{0:T(1024)S(1)} %pad_clamp_fusion), kind=kCustom, calls=%fused_computation | custom fusion | bytes 163872 | tf_op jit(solution)/shard_map/gather | solution.py:376
  9.6 5.8 %copy.22.out_hbm = bf16[5120,320]{1,0:T(8,128)(2,1)} copy(bf16[5120,320]{0,1:T(8,128)(2,1)} %param.21) | data formatting | bytes 6553600 | tf_op args[8]
  15.4 80.0 %shard_map.140 = (bf16[8,5120]{1,0:T(8,128)(2,1)}, bf16[8,320]{1,0:T(8,128)(2,1)}) custom-call(s32[2]{0:T(128)} %lengths.1, bf16[8,5120]{1,0:T(8,128)(2,1)} %gather_fusion, f32[8,1]{1,0:T(8,128)} %reshape.99.inside, f32[1,5120]{1,0:T(1,128)} %bitcast.5, f32[56,128]{1,0:T(8,128)} %bitcast.7, f32[8,128]{1,0:T(8,128)} %get-tuple-element.9.cos, ...), custom_call_target="tpu_custom_call" | custom-call | tf_op jit(solution)/shard_map/pallas_call | solution.py:389
  95.4 1.6 %reshape.86 = bf16[4,2,5120]{2,1,0:T(2,128)(2,1)} reshape(bf16[8,5120]{1,0:T(8,128)(2,1)} %get-tuple-element.4) | data formatting | bytes 163840 | tf_op jit(solution)/shard_map/reshape | solution.py:441
  97.0 1.3 %reshape.87 = bf16[4,2,320]{2,1,0:T(2,128)(2,1)} reshape(bf16[8,320]{1,0:T(8,128)(2,1)} %get-tuple-element.5) | data formatting | bytes 10240 | tf_op jit(solution)/shard_map/reshape | solution.py:442
  (3 shorter events, 0.0 us)

commit v2 on v1

--- a/solution.py
+++ b/solution.py
@@ -60,6 +60,9 @@
     narrow,
     down_out,
     down_in,
+    group_sum,
+    group_top,
+    group_total,
     load_sem,
     send_sem,
     recv_sem,
@@ -70,7 +73,7 @@
     tokens, width = picked.shape
     batches = keys.shape[0]
     local_len = keys.shape[1]
-    cols = w_out.shape[1]
+    cols = w_out.shape[0]
     joint_each = joint_out.shape[1]
     head_each = part_out.shape[1] - 1
     scale = 1.0 / math.sqrt(HEAD_DIM)
@@ -138,7 +141,7 @@
 
     wide[...] = picked[...].astype(F32) * inside[...]
     mean_square = jnp.sum(wide[...] * wide[...], axis=1, keepdims=True) / width
-    normed = (wide[...] * lax.rsqrt(mean_square + NORM_EPS) * gain_one[...]).astype(BF16)
+    normed = (wide[...] * lax.rsqrt(mean_square + NORM_EPS) * gain_one[...].astype(F32)[None, :]).astype(BF16)
     heads_out = jnp.concatenate([wide[...], normed.astype(F32)], axis=0)
     for j in range(n):
         rows_out[j] = heads_out[:, j * cols : (j + 1) * cols].astype(BF16)
@@ -156,7 +159,7 @@
     loads[0].wait()
     chunk = 4
 
-    @pl.loop(0, joint_heads // chunk)
+    @pl.loop(0, joint_heads // chunk, unroll=True)
     def _(c):
         part = jnp.dot(
             normed_local,
@@ -192,34 +195,32 @@
     loads[1].wait()
     loads[2].wait()
     group_rows = group * tokens
-    row_batch = lax.broadcasted_iota(jnp.int32, (group_rows, 1), 0) % batches
     places = me * local_len + lax.broadcasted_iota(jnp.int32, (1, local_len), 1)
     lane = lax.broadcasted_iota(jnp.int32, (tokens, HEAD_DIM), 1)
 
+    exponent = scale / math.log(2.0)
+
     @pl.loop(0, KV_HEADS)
     def _(k):
-        q = heads_wide[pl.ds(pl.multiple_of(k * group_rows, 8), group_rows), :].astype(BF16)
         head_cols = pl.ds(pl.multiple_of(k * HEAD_DIM, HEAD_DIM), HEAD_DIM)
-        top = total = summed = None
+        half = group_rows // batches
         for b in range(batches):
-            valid = places < lengths[b]
+            own_rows = pl.ds(b, half, stride=batches)
+            q = heads_wide[pl.ds(k * group_rows + b, half, stride=batches), :].astype(BF16)
             scores = lax.dot_general(
                 q, keys[b, :, head_cols], (((1,), (1,)), ((), ())), preferred_element_type=F32
             )
-            masked = jnp.where(valid, scores * scale, MASKED)
+            masked = jnp.where(places < lengths[b], scores, MASKED)
             own_top = jnp.max(masked, axis=1, keepdims=True)
-            weight = jnp.where(valid, jnp.exp(masked - own_top), 0.0)
+            weight = jnp.exp2((masked - own_top) * exponent)
             own_total = jnp.sum(weight, axis=1, keepdims=True)
             own_sum = jnp.dot(
                 weight.astype(BF16), values[b, :, head_cols], preferred_element_type=F32
             )
-            if b == 0:
-                top, total, summed = own_top, own_total, own_sum
-            else:
-                here = row_batch == b
-                top = jnp.where(here, own_top, top)
-                total = jnp.where(here, own_total, total)
-                summed = jnp.where(here, own_sum, summed)
+            group_sum[own_rows, :] = own_sum
+            group_top[own_rows, :] = jnp.broadcast_to(own_top * scale, own_sum.shape)
+            group_total[own_rows, :] = jnp.broadcast_to(own_total, own_sum.shape)
+        summed, top, total = group_sum[...], group_top[...], group_total[...]
         for g in range(group):
             h = k * group + g
             owner, slot = h // head_each, h % head_each
@@ -263,7 +264,7 @@
             )
 
         top = jnp.broadcast_to(top, (tokens, HEAD_DIM))
-        top = lax.fori_loop(0, n, lambda j, m: jnp.maximum(m, stat(j, 0)), top)
+        top = lax.fori_loop(0, n, lambda j, m: jnp.maximum(m, stat(j, 0)), top, unroll=True)
         total = jnp.zeros((tokens, HEAD_DIM), F32)
         summed = jnp.zeros((tokens, HEAD_DIM), F32)
         for t in range(tokens):
@@ -277,7 +278,7 @@
             factor = jnp.exp(stat(j, 0) - top)
             return total + stat(j, 1) * factor, summed + part_in[j, i] * factor
 
-        total, summed = lax.fori_loop(0, n, merge, (total, summed))
+        total, summed = lax.fori_loop(0, n, merge, (total, summed), unroll=True)
         tiles.append(summed / total)
     attended_all[me] = jnp.concatenate(tiles, axis=0).astype(BF16)
     send_all(4, attended_all, attended_all, False)
@@ -300,8 +301,14 @@
         0,
         width // depth,
         lambda c, acc: acc
-        + jnp.dot(narrow[:, piece(c)], w_out[piece(c), :], preferred_element_type=F32),
+        + lax.dot_general(
+            narrow[:, piece(c)],
+            w_out[:, piece(c)],
+            (((1,), (1,)), ((), ())),
+            preferred_element_type=F32,
+        ),
         jnp.zeros((tokens, cols), F32),
+        unroll=True,
     )
     mid_all[me] = mid
     send_all(5, mid_all, mid_all, False)
@@ -309,7 +316,7 @@
     for j in range(n):
         wide[:, j * cols : (j + 1) * cols] = mid_all[j]
     mean_square = jnp.sum(wide[...] * wide[...], axis=1, keepdims=True) / width
-    narrow[...] = (wide[...] * lax.rsqrt(mean_square + NORM_EPS) * gain_two[...]).astype(BF16)
+    narrow[...] = (wide[...] * lax.rsqrt(mean_square + NORM_EPS) * gain_two[...].astype(F32)[None, :]).astype(BF16)
 
     loads[4].wait()
     loads[5].wait()
@@ -324,11 +331,11 @@
         )
 
     zero = jnp.zeros((tokens, units), F32)
-    gate, upper = lax.fori_loop(0, width // depth, both, (zero, zero))
+    gate, upper = lax.fori_loop(0, width // depth, both, (zero, zero), unroll=True)
     hidden = (gate / (1.0 + jnp.exp(-gate)) * upper).astype(BF16)
     loads[6].wait()
 
-    @pl.loop(0, width // depth)
+    @pl.loop(0, width // depth, unroll=True)
     def _(c):
         wide[:, piece(c)] = jnp.dot(hidden, w_down[:, piece(c)], preferred_element_type=F32)
 
@@ -396,7 +403,7 @@
         out_specs=(vmem, vmem),
         scratch_shapes=[
             pltpu.VMEM(a.shape, a.dtype)
-            for a in (w_qkv, cache_keys, cache_values, w_out, w_gate, w_up, w_down)
+            for a in (w_qkv, cache_keys, cache_values, w_out.T, w_gate, w_up, w_down)
         ]
         + [
             pltpu.VMEM((n, 2 * tokens, cols), BF16),
@@ -413,6 +420,9 @@
             pltpu.VMEM((tokens, width), BF16),
             pltpu.VMEM((n, tokens, cols), F32),
             pltpu.VMEM((n, tokens, cols), F32),
+            pltpu.VMEM((HEADS // KV_HEADS * tokens, HEAD_DIM), F32),
+            pltpu.VMEM((HEADS // KV_HEADS * tokens, HEAD_DIM), F32),
+            pltpu.VMEM((HEADS // KV_HEADS * tokens, HEAD_DIM), F32),
             pltpu.SemaphoreType.DMA((7,)),
             pltpu.SemaphoreType.DMA((7, n)),
             pltpu.SemaphoreType.DMA((7, n)),
@@ -424,15 +434,15 @@
         lengths,
         picked,
         inside.astype(F32)[:, None],
-        attn_gain.astype(F32)[None, :],
+        attn_gain,
         qkv_bias.reshape(joint_heads, HEAD_DIM),
         cos,
         sin,
-        mlp_gain.astype(F32)[None, :],
+        mlp_gain,
         w_qkv,
         cache_keys,
         cache_values,
-        w_out,
+        w_out.T,
         w_gate,
         w_up,
         w_down,

time: 98.8 us -> 78.7 us (0.80)
  Pallas kernels: 80 us -> 68.4 us
  local copies, waits for them, and re-layouts: 12.2 us -> 6.37 us
  other arithmetic: 5.45 us -> 2.84 us
    pallas_call x1, Pallas kernels: 80 us -> 68.4 us  [body(): pl.pallas_call(functools.partial(layer_kernel, n), out_shape=(jax.ShapeDt...]
    unnamed x1 -> x0, local copies, waits for them, and re-layouts: 5.82 us -> none
    broadcast_in_dim x2 -> x0, other arithmetic: 2.6 us -> none  [the longest x1 1.3 us: body(): mlp_gain.astype(F32)[None, :]]
where the time goes in v2:
time: 78.7 us; the launch traced here: 78.2 us
  Pallas kernels  68.4 us (87%)
  local copies, waits for them, and re-layouts  6.37 us (8%)
  other arithmetic  2.84 us (4%)
    pallas_call x1, Pallas kernels, body(): pl.pallas_call(functools.partial(layer_kernel, n), out_shape=(jax.ShapeDt...  68.4 us
    gather x1, local copies, waits for them, and re-layouts, body(): embed_table.at[jnp.clip(local_ids, 0, vocab_rows - 1)]  2.49 us

profile of v2, /device:TPU:0, one launch (start us, length us, event | category | flops | bytes accessed | tf_op | source)
XLA Modules:
  0.0 78.2 jit_solution(10684319306363817651)
XLA Ops:
  0.6 0.7 and_convert_fusion
  1.3 0.7 subtract_clamp_fusion
  2.0 0.1 copy.18
  2.1 0.1 min.12
  2.2 0.1 copy.19
  2.3 0.7 reshape.97.inside
  3.0 0.7 add_convert_fusion
  3.6 0.1 convert_element_type.26
  3.7 0.1 fusion
  3.8 0.7 pad_maximum_fusion
  4.5 2.5 %gather_fusion = bf16[8,5120]{1,0:T(8,128)(2,1)} fusion(bf16[4752,5120]{1,0:T(8,128)(2,1)} %param.15, s32[1024]{0:T(1024)S(1)} %pad_clamp_fusion), kind=kCustom, calls=%fused_computation | custom fusion | bytes 163872 | tf_op jit(solution)/shard_map/gather | solution.py:383
  7.0 68.4 %shard_map.140 = (bf16[8,5120]{1,0:T(8,128)(2,1)}, bf16[8,320]{1,0:T(8,128)(2,1)}) custom-call(s32[2]{0:T(128)} %lengths.1, bf16[8,5120]{1,0:T(8,128)(2,1)} %gather_fusion, f32[8,1]{1,0:T(8,128)} %reshape.97.inside, bf16[5120]{0:T(1024)(128)(2,1)} %gain_one.1, f32[56,128]{1,0:T(8,128)} %bitcast.5, f32[8,128]{1,0:T(8,128)} %get-tuple-element.9.cos, ...), custom_call_target="tpu_custom_call" | custom-call | tf_op jit(solution)/shard_map/pallas_call | solution.py:396
  75.4 1.6 %reshape.86 = bf16[4,2,5120]{2,1,0:T(2,128)(2,1)} reshape(bf16[8,5120]{1,0:T(8,128)(2,1)} %get-tuple-element.4) | data formatting | bytes 163840 | tf_op jit(solution)/shard_map/reshape | solution.py:451
  76.9 1.3 %reshape.87 = bf16[4,2,320]{2,1,0:T(2,128)(2,1)} reshape(bf16[8,320]{1,0:T(8,128)(2,1)} %get-tuple-element.5) | data formatting | bytes 10240 | tf_op jit(solution)/shard_map/reshape | solution.py:452
  (3 shorter events, 0.0 us)
